TPU v7x, 32 devices: a whole 2x2x4 slice. The times are simulated.
32 devices in a mesh: row: 2 (over x), col: 16 (over z, y, core).
Axes of the slice: x: 2, y: 2, z: 4, core: 2. Of those that a mesh axis runs over, the one named last changes fastest.
Arguments:
- matrix: bfloat16 [1024, 65536], P('row', 'col'), may hold values from -0.1875 to 0.1875
- measured: float32 [256, 1024], P(None, 'row'), may hold values from -160 to 160
- support: int32 [4, 1024], replicated, may hold values from 0 to 65535, as said below
Outputs:
- estimate: float32 [256, 65536], P('row', 'col')
- row_norms: float32 [65536], P('col')
- residual_energy: float32 [4], replicated
Inputs may be any that keep to these rules, and one draw needn't show every extreme that they name: Each row of support lists 1024 distinct signal-row indices in increasing order; in every row, each aligned block of 4096 indices (the signal rows of one index of col) holds at most 128 of them, and some block exactly 128.
All inputs are finite; a program needn't handle non-finite values.
Results may differ from a plain program's by a relative error of at most 0.015.
Values may be sent and summed in bfloat16 or wider, within the bound.
A program may use at most 64 MiB of HBM per device.

v0:
```python
import jax
import jax.numpy as jnp
from jax import lax
from jax.sharding import PartitionSpec as P

KMAX = 128


STEP_SIZE = 0.25


def local_support(support_row, start_col, block_width):
    below_count = jnp.sum((support_row < start_col).astype(jnp.int32))
    inside = jnp.sum(
        ((support_row >= start_col) & (support_row < start_col + block_width)).astype(jnp.int32)
    )
    padded = jnp.concatenate([support_row, jnp.full((KMAX,), start_col + block_width, jnp.int32)])
    window = lax.dynamic_slice_in_dim(padded, below_count, KMAX) - start_col
    occupied = jnp.arange(KMAX) < inside
    take_index = jnp.where(occupied, window, 0)
    drop_index = jnp.where(occupied, window, block_width)
    return (take_index, drop_index, occupied)


def dense_step(current, residual_half, matrix, drop_index):
    gradient = lax.psum_scatter(
        jnp.dot(residual_half, matrix, preferred_element_type=jnp.float32).astype(jnp.bfloat16),
        "row",
        scatter_dimension=0,
        tiled=True,
    ).astype(jnp.float32)
    stepped = current + STEP_SIZE * gradient
    keep_mask = jnp.zeros((current.shape[1],), jnp.float32).at[drop_index].set(1.0, mode="drop")
    return (stepped, stepped * keep_mask[None, :])


def local(matrix, measured, support):
    signals = measured.shape[0]
    rows_mine = signals // lax.axis_size("row")
    columns = matrix.shape[1]
    offset = lax.axis_index("col") * columns
    iterations = support.shape[0]
    total_count = signals * measured.shape[1] * lax.axis_size("row")
    current = jnp.zeros((rows_mine, columns), jnp.float32)
    stepped = current
    energies = []
    for iteration in range(iterations):
        if iteration == 0:
            residual = measured
        else:
            current_half = current.astype(jnp.bfloat16)
            take_before, drop_before, occupied_before = local_support(
                support[iteration - 1], offset, columns
            )
            kept_matrix = jnp.where(
                occupied_before[None, :],
                jnp.take(matrix, take_before, axis=1),
                jnp.zeros((), jnp.bfloat16),
            )
            kept_current = jnp.take(current_half, take_before, axis=1)
            partial_image = lax.dot_general(
                lax.all_gather(kept_current, "row", axis=0, tiled=True),
                kept_matrix,
                (((1,), (1,)), ((), ())),
                preferred_element_type=jnp.float32,
            )
            predicted = lax.psum(partial_image.astype(jnp.bfloat16), "col").astype(jnp.float32)
            residual = measured - predicted
        local_energy = jnp.sum(residual * residual)
        energies.append(lax.psum(local_energy, "row"))
        residual_half = residual.astype(jnp.bfloat16)
        take_index, drop_index, occupied = local_support(support[iteration], offset, columns)
        stepped, current = dense_step(current, residual_half, matrix, drop_index)
    row_local = jnp.sum(stepped * stepped, axis=0)
    column_energy = lax.psum(row_local, "row")
    residual_sums = jnp.stack(energies)
    return (current, jnp.sqrt(column_energy), residual_sums / total_count)


def solution(mesh):
    placed = (P("row", "col"), P(None, "row"), P())
    return jax.shard_map(
        local,
        mesh=mesh,
        in_specs=placed,
        out_specs=(P("row", "col"), P("col"), P()),
        check_vma=False,
    )
```

profile of v0, /device:TPU:0, one launch (start us, length us, event | category | flops | bytes accessed | tf_op | source)
XLA Modules:
  0.0 480.0 jit_solution(8666434360889292542)
XLA Ops:
  7.2 4.9 %convolution_convert_fusion.3 = bf16[256,4096]{1,0:T(8,128)(2,1)} fusion(bf16[512,4096]{1,0:T(8,128)(2,1)} %param.7, f32[256,512]{1,0:T(8,128)} %param.8), kind=kOutput, calls=%fused_computation.13 | convolution fusion | flops 1074921472 | bytes 6815744 | tf_op jit(solution)/shard_map/dot_general | solution.py:27
  12.2 6.5 %copy.7 = bf16[512,4096]{0,1:T(8,128)(2,1)} copy(bf16[512,4096]{1,0:T(8,128)(2,1)} %param.7) | data formatting | bytes 8388608 | tf_op args[0]
  22.1 3.6 gather_fusion.1
  26.3 1.0 scatter_custom_fusion
  28.0 18.9 %reduce-scatter.5.cloned.1.call-done = bf16[128,4096]{1,0:T(8,128)(2,1)} async-done(((bf16[256,4096]{1,0:T(8,128)(2,1)}), bf16[128,4096]{1,0:T(8,128)(2,1)}) %reduce-scatter.5.cloned.1.call-update) | async-done | bytes 1048592 | tf_op jit(solution)/shard_map/reduce_scatter | solution.py:26
  47.0 1.4 fusion
  49.9 4.6 all_gather.9
  54.5 1.0 convolution_convert_fusion.6
  55.6 89.8 %all-reduce.9.cloned.1.call-done = bf16[256,512]{1,0:T(8,128)(2,1)} async-done(((bf16[256,512]{1,0:T(8,128)(2,1)}), bf16[256,512]{1,0:T(8,128)(2,1)}) %all-reduce.9.cloned.1.call-update) | async-done | bytes 262160 | tf_op jit(solution)/shard_map/psum | solution.py:67
  145.4 4.9 %convolution_convert_fusion.2 = bf16[256,4096]{1,0:T(8,128)(2,1)} fusion(bf16[512,4096]{1,0:T(8,128)(2,1)} %param.7, f32[256,512]{1,0:T(8,128)S(1)} %copy-done.3, bf16[256,512]{1,0:T(8,128)(2,1)} %all-reduce.9.cloned.1.call-done), kind=kOutput, calls=%fused_computation.12 | convolution fusion | flops 1075183616 | bytes 7077888 | tf_op jit(solution)/shard_map/dot_general | solution.py:27
  155.3 4.2 gather_fusion.3
  160.2 22.6 %reduce-scatter.7.cloned.1.call-done = bf16[128,4096]{1,0:T(8,128)(2,1)} async-done(((bf16[256,4096]{1,0:T(8,128)(2,1)}), bf16[128,4096]{1,0:T(8,128)(2,1)}) %reduce-scatter.7.cloned.1.call-update) | async-done | bytes 1048592 | tf_op jit(solution)/shard_map/reduce_scatter | solution.py:26
  182.8 1.7 fusion.1
  186.0 4.6 all_gather.10
  190.6 1.0 convolution_convert_fusion.5
  191.7 89.8 %all-reduce.11.cloned.1.call-done = bf16[256,512]{1,0:T(8,128)(2,1)} async-done(((bf16[256,512]{1,0:T(8,128)(2,1)}), bf16[256,512]{1,0:T(8,128)(2,1)}) %all-reduce.11.cloned.1.call-update) | async-done | bytes 262160 | tf_op jit(solution)/shard_map/psum | solution.py:67
  281.5 5.0 %convolution_convert_fusion.1 = bf16[256,4096]{1,0:T(8,128)(2,1)} fusion(bf16[512,4096]{1,0:T(8,128)(2,1)} %param.7, f32[256,512]{1,0:T(8,128)} %param.8, bf16[256,512]{1,0:T(8,128)(2,1)} %all-reduce.11.cloned.1.call-done), kind=kOutput, calls=%fused_computation.11 | convolution fusion | flops 1075183616 | bytes 7077888 | tf_op jit(solution)/shard_map/dot_general | solution.py:27
  290.5 1.2 scatter_custom_fusion.2
  291.7 4.3 gather_fusion.5
  296.7 22.4 %reduce-scatter.9.cloned.1.call-done = bf16[128,4096]{1,0:T(8,128)(2,1)} async-done(((bf16[256,4096]{1,0:T(8,128)(2,1)}), bf16[128,4096]{1,0:T(8,128)(2,1)}) %reduce-scatter.9.cloned.1.call-update) | async-done | bytes 1048592 | tf_op jit(solution)/shard_map/reduce_scatter | solution.py:26
  319.1 1.9 fusion.42
  321.0 1.3 copy.10
  322.3 2.0 gather_fusion.4
  324.4 4.6 all_gather.11
  329.0 1.0 convolution_convert_fusion.4
  330.1 89.9 %all-reduce.13.cloned.1.call-done = bf16[256,512]{1,0:T(8,128)(2,1)} async-done(((bf16[256,512]{1,0:T(8,128)(2,1)}), bf16[256,512]{1,0:T(8,128)(2,1)}) %all-reduce.13.cloned.1.call-update) | async-done | bytes 262160 | tf_op jit(solution)/shard_map/psum | solution.py:67
  420.0 5.0 %convolution_convert_fusion = bf16[256,4096]{1,0:T(8,128)(2,1)} fusion(bf16[512,4096]{1,0:T(8,128)(2,1)} %param.7, f32[256,512]{1,0:T(8,128)} %param.8, bf16[256,512]{1,0:T(8,128)(2,1)} %all-reduce.13.cloned.1.call-done), kind=kOutput, calls=%fused_computation.10 | convolution fusion | flops 1075183616 | bytes 7077888 | tf_op jit(solution)/shard_map/dot_general | solution.py:27
  429.3 2.1 multiply_reduce_fusion.4
  431.4 26.2 %reduce-scatter.11.cloned.1.call-done = bf16[128,4096]{1,0:T(8,128)(2,1)} async-done(((bf16[256,4096]{1,0:T(8,128)(2,1)}), bf16[128,4096]{1,0:T(8,128)(2,1)}) %reduce-scatter.11.cloned.1.call-update) | async-done | bytes 1048592 | tf_op jit(solution)/shard_map/reduce_scatter | solution.py:26
  457.6 3.6 multiply_reduce_fusion
  461.2 8.2 %all-reduce.4 = (f32[4096]{0:T(1024)S(1)}, f32[1]{0:T(128)}, f32[1]{0:T(128)}, f32[1]{0:T(128)}, f32[1]{0:T(128)}) all-reduce(f32[4096]{0:T(1024)S(1)} %get-tuple-element.31, f32[1]{0:T(128)} %bitcast.13, f32[1]{0:T(128)} %bitcast.12, f32[1]{0:T(128)} %bitcast.11, f32[1]{0:T(128)} %bitcast.10), channel_id=1, replica_groups=mesh['row'=2,'col'=16] {'row'}, use_global_device_ids=true, to_apply=%region_20.23 | all-reduce | flops 4100 | bytes 32800 | tf_op jit(solution)/shard_map/psum | solution.py:75
  470.1 3.1 maximum_multiply_fusion
  (56 shorter events, 15.5 us)
Async XLA Ops:
  7.2 39.8 %reduce-scatter.5.cloned.1.call-start = ((), (), s32[]{:S(2)}) async-start(), calls=%async_computation.4 | async-start | bytes 3145728 | tf_op jit(solution)/shard_map/reduce_scatter | solution.py:26
  12.2 133.2 %all-reduce.9.cloned.1.call-start = ((), (), s32[]{:S(2)}) async-start(), calls=%async_computation.5 | async-start | bytes 524288 | tf_op jit(solution)/shard_map/psum | solution.py:67
  12.2 6.5 %copy-start.5 = (s32[4,1024]{1,0:T(4,128)S(1)}, s32[4,1024]{1,0:T(4,128)}, u32[]{:S(2)}) copy-start(s32[4,1024]{1,0:T(4,128)} %param.9) | copy-start | bytes 49156
  48.4 97.0 %copy-start.3 = (f32[256,512]{1,0:T(8,128)S(1)}, f32[256,512]{1,0:T(8,128)}, u32[]{:S(2)}) copy-start(f32[256,512]{1,0:T(8,128)} %param.8) | copy-start | bytes 1572868
  55.5 127.3 %reduce-scatter.7.cloned.1.call-start = ((), (), s32[]{:S(2)}) async-start(), calls=%async_computation.6 | async-start | bytes 3145728 | tf_op jit(solution)/shard_map/reduce_scatter | solution.py:26
  150.3 32.6 %copy-start = (bf16[128,4096]{1,0:T(8,128)(2,1)S(1)}, bf16[128,4096]{1,0:T(8,128)(2,1)}, u32[]{:S(2)}) copy-start(bf16[128,4096]{1,0:T(8,128)(2,1)} %reduce-scatter.5.cloned.1.call-done) | copy-start | bytes 3145732
  150.3 131.2 %all-reduce.11.cloned.1.call-start = ((), (), s32[]{:S(2)}) async-start(), calls=%async_computation.7 | async-start | bytes 524288 | tf_op jit(solution)/shard_map/psum | solution.py:67
  191.6 127.4 %reduce-scatter.9.cloned.1.call-start = ((), (), s32[]{:S(2)}) async-start(), calls=%async_computation.8 | async-start | bytes 3145728 | tf_op jit(solution)/shard_map/reduce_scatter | solution.py:26
  286.5 32.6 %copy-start.1 = (bf16[128,4096]{1,0:T(8,128)(2,1)S(1)}, bf16[128,4096]{1,0:T(8,128)(2,1)}, u32[]{:S(2)}) copy-start(bf16[128,4096]{1,0:T(8,128)(2,1)} %reduce-scatter.7.cloned.1.call-done) | copy-start | bytes 3145732
  286.5 133.4 %all-reduce.13.cloned.1.call-start = ((), (), s32[]{:S(2)}) async-start(), calls=%async_computation.9 | async-start | bytes 524288 | tf_op jit(solution)/shard_map/psum | solution.py:67
  330.0 127.6 %reduce-scatter.11.cloned.1.call-start = ((), (), s32[]{:S(2)}) async-start(), calls=%async_computation.10 | async-start | bytes 3145728 | tf_op jit(solution)/shard_map/reduce_scatter | solution.py:26
  425.0 4.3 copy-start.4
  425.0 32.6 %copy-start.2 = (bf16[128,4096]{1,0:T(8,128)(2,1)S(1)}, bf16[128,4096]{1,0:T(8,128)(2,1)}, u32[]{:S(2)}) copy-start(bf16[128,4096]{1,0:T(8,128)(2,1)} %reduce-scatter.9.cloned.1.call-done) | copy-start | bytes 3145732
Sparse Core Ops, SparseCore 0:
  12.3 34.6 reduce-scatter.4
  55.6 89.7 all-reduce.8
  150.4 32.3 reduce-scatter.6
  191.7 89.6 all-reduce.10
  286.6 32.3 reduce-scatter.8
  330.2 89.7 all-reduce.12
  425.1 32.4 reduce-scatter.10
where the time goes:
time: 481 us; the launch traced here: 480 us
  waiting for transfers between devices  360 us (75%)
  local copies, waits for them, and re-layouts  29.5 us (6%)
  other arithmetic  23.5 us (5%)
  matrix products  22.9 us (5%)
  blocking collectives  22.1 us (5%)
  between operations  22.1 us (5%)
    psum x3, waiting for transfers between devices, local(): lax.psum(partial_image.astype(jnp.bfloat16), 'col').astype(jnp.float32)  269 us
    reduce_scatter x4, waiting for transfers between devices, dense_step(): lax.psum_scatter(jnp.dot(residual_half, matrix, preferred_element_type=jn...  90.1 us
    dot_general x4, matrix products, dense_step(): jnp.dot(residual_half, matrix, preferred_element_type=jnp.float32)  19.8 us
    all_gather x3, blocking collectives, local(): lax.all_gather(kept_current, 'row', axis=0, tiled=True)  13.8 us
    gather x3, local copies, waits for them, and re-layouts, local(): jnp.take(matrix, take_before, axis=1)  12.1 us
  transfers between devices with their start and end apart: 7, of which 7 were waited for; matrix products, arithmetic and copies ran while one was open for 7% of the time, Pallas kernels for 0%

commit v1 on v0

v1 whole, which is shorter than its diff:
```python
import jax
import jax.numpy as jnp
from jax import lax
from jax.sharding import PartitionSpec as P

KMAX = 128
STEP_SIZE = 0.25
HI = lax.Precision.HIGHEST
NT = (((1,), (1,)), ((), ()))


def window(support_row, start, width):
    below = jnp.sum((support_row < start).astype(jnp.int32))
    local = support_row - start
    inside = (local >= 0) & (local < width)
    slot = jnp.arange(support_row.shape[0]) - below
    chosen = (slot[None, :] == jnp.arange(KMAX)[:, None]) & inside[None, :]
    return jnp.sum(jnp.where(chosen, local[None, :] + 1, 0), axis=1) - 1


def local(matrix, measured, support):
    signals = measured.shape[0]
    n_row = lax.axis_size("row")
    rows_mine = signals // n_row
    columns = matrix.shape[1]
    offset = lax.axis_index("col") * columns
    iterations = support.shape[0]
    total_count = signals * measured.shape[1] * n_row
    lanes = jnp.arange(columns)
    index = [window(support[t], offset, columns) for t in range(iterations)]
    onehot = [(i[:, None] == lanes[None, :]).astype(jnp.bfloat16) for i in index]
    kept = [
        lax.dot_general(e, matrix, NT, preferred_element_type=jnp.float32).astype(jnp.bfloat16)
        for e in onehot[:-1]
    ]
    residual = measured
    current = jnp.zeros((signals, KMAX), jnp.float32)
    energies = []
    for t in range(iterations):
        energies.append(jnp.sum(residual * residual))
        half = residual.astype(jnp.bfloat16)
        if t == iterations - 1:
            break
        part = lax.dot_general(half, kept[t], NT, preferred_element_type=jnp.float32)
        gradient = lax.psum(part.astype(jnp.bfloat16), "row").astype(jnp.float32)
        if t:
            same = (index[t - 1][:, None] == index[t][None, :]) & (index[t] >= 0)[None, :]
            current = jnp.dot(current, same.astype(jnp.float32), precision=HI)
        current = current + STEP_SIZE * gradient
        image = jnp.dot(current.astype(jnp.bfloat16), kept[t], preferred_element_type=jnp.float32)
        residual = measured - lax.psum(image.astype(jnp.bfloat16), "col").astype(jnp.float32)
    gradient = lax.psum_scatter(
        jnp.dot(half, matrix, preferred_element_type=jnp.float32).astype(jnp.bfloat16),
        "row", scatter_dimension=0, tiled=True,
    ).astype(jnp.float32)
    mine = lax.dynamic_slice_in_dim(current, lax.axis_index("row") * rows_mine, rows_mine, 0)
    stepped = jnp.dot(mine, onehot[-2].astype(jnp.float32), precision=HI) + STEP_SIZE * gradient
    keep = jnp.sum(onehot[-1].astype(jnp.float32), axis=0)
    sums = jnp.concatenate([jnp.sum(stepped * stepped, axis=0), jnp.stack(energies)])
    sums = lax.psum(sums, "row")
    return (stepped * keep[None, :], jnp.sqrt(sums[:columns]), sums[columns:] / total_count)


def solution(mesh):
    placed = (P("row", "col"), P(None, "row"), P())
    return jax.shard_map(
        local,
        mesh=mesh,
        in_specs=placed,
        out_specs=(P("row", "col"), P("col"), P()),
        check_vma=False,
    )
```

time: 481 us -> 429 us (0.89)
  local copies, waits for them, and re-layouts: 29.5 us -> 3.8 us
  other arithmetic: 23.5 us -> 7.66 us
  blocking collectives: 22.1 us -> 7.1 us
  between operations: 22.1 us -> 14.2 us
  matrix products: 22.9 us -> 30.6 us
    psum x3 -> x6, waiting for transfers between devices: 269 us -> 334 us  [the longest x3 269 us: local(): lax.psum(image.astype(jnp.bfloat16), 'col').astype(jnp.float32)]
    reduce_scatter x4 -> x1, waiting for transfers between devices: 90.1 us -> 30.5 us  [local(): lax.psum_scatter(jnp.dot(half, matrix, preferred_element_type=jnp.float32...]
    gather x6 -> x0, local copies, waits for them, and re-layouts: 15.5 us -> none  [the longest x3 12.1 us: local(): jnp.take(matrix, take_before, axis=1)]
    all_gather x3 -> x0, blocking collectives: 13.8 us -> none  [local(): lax.all_gather(kept_current, 'row', axis=0, tiled=True)]
    dot_general x7 -> x13, matrix products: 22.9 us -> 30.6 us  [the longest x3 11.1 us: local(): lax.dot_general(e, matrix, NT, preferred_element_type=jnp.float32)]
    reduce_sum x6, other arithmetic: 8.29 us -> 2.01 us  [the longest x1 0.94 us: local(): energies.append(jnp.sum(residual * residual))]
    unnamed x13 -> x8, local copies, waits for them, and re-layouts: 6.5 us -> 0.56 us
    convert_element_type x3 -> x0, other arithmetic: 5.03 us -> none  [local(): current_half = current.astype(jnp.bfloat16)]
  transfers between devices with their start and end apart: 7 -> 7, of which waited for: 7 -> 7; matrix products, arithmetic and copies ran while one was open for 7% -> 2% of each run, Pallas kernels for 0% -> 0%
where the time goes in v1:
time: 429 us; the launch traced here: 428 us
  waiting for transfers between devices  364 us (85%)
  matrix products  30.6 us (7%)
  between operations  14.2 us (3%)
  other arithmetic  7.66 us (2%)
  blocking collectives  7.1 us (2%)
    psum x3, waiting for transfers between devices, local(): lax.psum(image.astype(jnp.bfloat16), 'col').astype(jnp.float32)  269 us
    psum x3, waiting for transfers between devices, local(): gradient = lax.psum(part.astype(jnp.bfloat16), 'row').astype(jnp.float32)  64.5 us
    reduce_scatter x1, waiting for transfers between devices, local(): lax.psum_scatter(jnp.dot(half, matrix, preferred_element_type=jnp.float32...  30.5 us
    dot_general x3, matrix products, local(): lax.dot_general(e, matrix, NT, preferred_element_type=jnp.float32)  11.1 us
  transfers between devices with their start and end apart: 7, of which 7 were waited for; matrix products, arithmetic and copies ran while one was open for 2% of the time, Pallas kernels for 0%

profile of v1, /device:TPU:0, one launch (start us, length us, event | category | flops | bytes accessed | tf_op | source)
XLA Modules:
  0.0 428.1 jit_solution(17295335813921915850)
XLA Ops:
  7.2 0.9 and_reduce_fusion
  8.2 1.6 subtract_add_fusion
  9.8 1.3 iota_subtract_fusion.2
  11.3 3.8 fusion.5
  15.0 0.9 fusion.7
  16.2 3.7 fusion.4
  19.9 19.9 %all-reduce.7.cloned.1.call-done = bf16[256,128]{0,1:T(8,128)(2,1)} async-done(((bf16[256,128]{0,1:T(8,128)(2,1)}), bf16[256,128]{0,1:T(8,128)(2,1)}) %all-reduce.7.cloned.1.call-update) | async-done | bytes 65552 | tf_op jit(solution)/shard_map/psum | solution.py:45
  39.8 1.8 convolution_convert_fusion.3
  41.6 1.3 iota_subtract_fusion
  42.9 0.2 select_reduce_fusion.1
  43.1 90.4 %all-reduce.9.cloned.1.call-done = bf16[256,512]{1,0:T(8,128)(2,1)} async-done(((bf16[256,512]{1,0:T(8,128)(2,1)}), bf16[256,512]{1,0:T(8,128)(2,1)}) %all-reduce.9.cloned.1.call-update) | async-done | bytes 262160 | tf_op jit(solution)/shard_map/psum | solution.py:51
  133.4 1.8 convolution_convert_fusion.5
  135.3 22.4 %all-reduce.11.cloned.1.call-done = bf16[256,128]{0,1:T(8,128)(2,1)} async-done(((bf16[256,128]{0,1:T(8,128)(2,1)}), bf16[256,128]{0,1:T(8,128)(2,1)}) %all-reduce.11.cloned.1.call-update) | async-done | bytes 65552 | tf_op jit(solution)/shard_map/psum | solution.py:45
  157.7 1.2 convolution_add_fusion.2
  158.9 1.0 convolution_convert_fusion.2
  160.0 3.7 fusion.6
  163.7 87.6 %all-reduce.13.cloned.1.call-done = bf16[256,512]{1,0:T(8,128)(2,1)} async-done(((bf16[256,512]{1,0:T(8,128)(2,1)}), bf16[256,512]{1,0:T(8,128)(2,1)}) %all-reduce.13.cloned.1.call-update) | async-done | bytes 262160 | tf_op jit(solution)/shard_map/psum | solution.py:51
  251.3 1.8 convolution_convert_fusion.4
  253.2 22.2 %all-reduce.15.cloned.1.call-done = bf16[256,128]{0,1:T(8,128)(2,1)} async-done(((bf16[256,128]{0,1:T(8,128)(2,1)}), bf16[256,128]{0,1:T(8,128)(2,1)}) %all-reduce.15.cloned.1.call-update) | async-done | bytes 65552 | tf_op jit(solution)/shard_map/psum | solution.py:45
  275.4 1.2 convolution_add_fusion.1
  276.6 1.0 convolution_convert_fusion.1
  277.6 91.3 %all-reduce.17.cloned.1.call-done = bf16[256,512]{1,0:T(8,128)(2,1)} async-done(((bf16[256,512]{1,0:T(8,128)(2,1)}), bf16[256,512]{1,0:T(8,128)(2,1)}) %all-reduce.17.cloned.1.call-update) | async-done | bytes 262160 | tf_op jit(solution)/shard_map/psum | solution.py:51
  368.9 4.9 %convolution_convert_fusion = bf16[256,4096]{1,0:T(8,128)(2,1)} fusion(bf16[512,4096]{1,0:T(8,128)(2,1)} %param.3, f32[256,512]{1,0:T(8,128)S(1)} %copy-done, bf16[256,512]{1,0:T(8,128)(2,1)} %all-reduce.17.cloned.1.call-done), kind=kOutput, calls=%fused_computation | convolution fusion | flops 1075183616 | bytes 7077888 | tf_op jit(solution)/shard_map/dot_general | solution.py:53
  374.0 0.3 convert_reduce_fusion
  374.3 0.4 copy-done.1
  374.9 0.9 multiply_reduce_fusion.1
  375.8 30.5 %reduce-scatter.2.cloned.1.call-done = bf16[128,4096]{1,0:T(8,128)(2,1)} async-done(((bf16[256,4096]{1,0:T(8,128)(2,1)}), bf16[128,4096]{1,0:T(8,128)(2,1)}) %reduce-scatter.2.cloned.1.call-update) | async-done | bytes 1048592 | tf_op jit(solution)/shard_map/reduce_scatter | solution.py:52
  406.4 4.1 multiply_reduce_fusion
  410.4 2.6 concatenate.3
  413.1 7.1 %psum.55 = f32[4100]{0:T(1024)S(1)} all-reduce(f32[4100]{0:T(1024)S(1)} %concatenate.3), channel_id=1, replica_groups=mesh['row'=2,'col'=16] {'row'}, use_global_device_ids=true, to_apply=%region_21.22 | all-reduce | flops 4100 | bytes 32800 | tf_op jit(solution)/shard_map/psum | solution.py:60
  420.2 0.5 slice_multiply_fusion
  420.7 0.6 slice_sqrt_fusion
  (30 shorter events, 1.2 us)
Async XLA Ops:
  7.2 32.6 %all-reduce.7.cloned.1.call-start = ((), (), s32[]{:S(2)}) async-start(), calls=%async_computation.1 | async-start | bytes 131072 | tf_op jit(solution)/shard_map/psum | solution.py:45
  11.3 3.8 copy-start
  15.9 117.5 %all-reduce.9.cloned.1.call-start = ((), (), s32[]{:S(2)}) async-start(), calls=%async_computation.2 | async-start | bytes 524288 | tf_op jit(solution)/shard_map/psum | solution.py:51
  41.6 116.1 %all-reduce.11.cloned.1.call-start = ((), (), s32[]{:S(2)}) async-start(), calls=%async_computation.3 | async-start | bytes 131072 | tf_op jit(solution)/shard_map/psum | solution.py:45
  135.3 116.0 %all-reduce.13.cloned.1.call-start = ((), (), s32[]{:S(2)}) async-start(), calls=%async_computation.4 | async-start | bytes 524288 | tf_op jit(solution)/shard_map/psum | solution.py:51
  159.9 115.5 %all-reduce.15.cloned.1.call-start = ((), (), s32[]{:S(2)}) async-start(), calls=%async_computation.5 | async-start | bytes 131072 | tf_op jit(solution)/shard_map/psum | solution.py:45
  253.1 115.8 %all-reduce.17.cloned.1.call-start = ((), (), s32[]{:S(2)}) async-start(), calls=%async_computation.6 | async-start | bytes 524288 | tf_op jit(solution)/shard_map/psum | solution.py:51
  277.5 128.8 %reduce-scatter.2.cloned.1.call-start = ((), (), s32[]{:S(2)}) async-start(), calls=%async_computation.7 | async-start | bytes 3145728 | tf_op jit(solution)/shard_map/reduce_scatter | solution.py:52
  373.8 0.9 copy-start.1
  373.8 1.0 copy-start.2
  373.8 1.1 copy-start.3
Sparse Core Ops, SparseCore 0:
  16.0 23.6 all-reduce.6
  43.7 89.6 all-reduce.8
  136.3 21.4 all-reduce.10
  161.5 89.6 all-reduce.12
  253.9 21.4 all-reduce.14
  279.2 89.6 all-reduce.16
  373.9 32.3 reduce-scatter.1

commit v2 on v1

v2 whole, which is shorter than its diff:
```python
import functools

import jax
import jax.numpy as jnp
from jax import lax
from jax.experimental import pallas as pl
from jax.experimental.pallas import tpu as pltpu
from jax.sharding import PartitionSpec as P

KMAX = 128
STEP_SIZE = 0.25
LANES = 128
NT = (((1,), (1,)), ((), ()))
F32, BF16 = jnp.float32, jnp.bfloat16
MESH = pl.DeviceIdType.MESH


def dot(a, b):
    return jnp.dot(a, b, preferred_element_type=F32)


def dot_nt(a, b):
    return lax.dot_general(a, b, NT, preferred_element_type=F32)


def pick(values, onehot):
    high = values.astype(BF16)
    rest = values - high.astype(F32)
    mid = rest.astype(BF16)
    low = (rest - mid.astype(F32)).astype(BF16)
    return dot(high, onehot) + dot(mid, onehot) + dot(low, onehot)


def iota(shape, axis):
    return lax.broadcasted_iota(jnp.int32, shape, axis).astype(F32)


def kernel(n_row, n_col, mat, meas, sup, est, norms, energy,
           kept, g0_send, g0_recv, yshard, big, pfull, pair_in, rs_out, rs_in,
           rall, rrows, en_out, en_in, fin_out, fin_in,
           kept_s, kept_r, g0_s, g0_r, y_s, y_r, big_s, big_r, loc,
           pair_s, pair_r, rs_s, rs_r, ag_s, ag_r, rel_s, rel_r, rx_s, rx_r,
           en_s, en_r, fin_s, fin_r):
    r, c = lax.axis_index("row"), lax.axis_index("col")
    n_chip = n_col // 2
    q, h = lax.rem(c, 2), lax.div(c, 2)
    mate = h * 2 + (1 - q)
    mb, width = mat.shape
    signals = meas.shape[0]
    iters, total_k = sup.shape
    ls = signals // n_row
    lh = ls // 2
    msh = mb * n_row // n_chip
    wq = width // n_row
    per = mb // msh

    def remote(src, dst, s, d, row=None, col=None):
        return pltpu.make_async_remote_copy(
            src_ref=src, dst_ref=dst, send_sem=s, recv_sem=d,
            device_id=(r if row is None else row, c if col is None else col),
            device_id_type=MESH)

    barrier = pltpu.get_barrier_semaphore()
    for p in range(1, n_row):
        pl.semaphore_signal(barrier, inc=1, device_id=(lax.rem(r + p, n_row), c), device_id_type=MESH)
    for p in range(1, n_col):
        pl.semaphore_signal(barrier, inc=1, device_id=(r, lax.rem(c + p, n_col)), device_id_type=MESH)

    own_big = pltpu.make_async_copy(mat.at[:, pl.ds(pl.multiple_of(r * wq, LANES), wq)], big.at[r], loc)
    own_big.start()

    offset = (c * width).astype(F32)
    eye = iota((KMAX, KMAX), 0) == iota((KMAX, KMAX), 1)
    index = []
    for t in range(iters):
        local = sup[t:t + 1, :].astype(F32) - offset
        below = jnp.sum(jnp.where(local < 0, 1.0, 0.0), axis=1, keepdims=True)
        slot = iota((1, total_k), 1) - below
        slot = jnp.where((local >= 0) & (local < width), slot, -1.0)
        hit = slot == iota((KMAX, total_k), 0)
        index.append(jnp.max(jnp.where(hit, local, -1.0), axis=1, keepdims=True))

    def onehot(t):
        return jnp.where(index[t] == iota((KMAX, width), 1), 1.0, 0.0).astype(BF16)

    def carried(values, t):
        as_row = jnp.sum(jnp.where(eye, index[t + 1], 0.0), axis=0, keepdims=True)
        same = jnp.where((index[t] == as_row) & (as_row >= 0), 1.0, 0.0).astype(BF16)
        return pick(values, same)

    copies = []

    def gather_kept(t):
        kept[t, r] = dot_nt(onehot(t), mat[...]).astype(BF16)

    def send_kept(t):
        out = []
        for p in range(1, n_row):
            k = remote(kept.at[t, r], kept.at[t, r], kept_s.at[t, p - 1], kept_r.at[t, p - 1],
                       row=lax.rem(r + p, n_row))
            k.start()
            out.append(k)
        return out

    gather_kept(0)
    part = dot_nt(meas[...].astype(BF16), kept[0, r])
    for rr in range(n_row):
        g0_send[rr] = part[rr * ls:(rr + 1) * ls].astype(BF16)
    energy0 = jnp.sum(jnp.sum(meas[...] * meas[...], axis=1, keepdims=True), axis=0, keepdims=True)

    pl.semaphore_wait(barrier, n_row + n_col - 2)

    g0 = []
    for p in range(1, n_row):
        rr = lax.rem(r + p, n_row)
        k = remote(g0_send.at[rr], g0_recv.at[p - 1], g0_s.at[p - 1], g0_r.at[p - 1], row=rr)
        k.start()
        g0.append(k)
    kept_copies = [send_kept(0)]
    holder = lax.div(h * msh, mb)
    yoff = pl.multiple_of(lax.rem(h * msh, mb), LANES)

    def y_copy(p):
        rr = lax.rem(r + p, n_row)
        rows = pl.ds(pl.multiple_of(rr * ls + q * lh, 8), lh)
        return remote(meas.at[rows, pl.ds(yoff, msh)], yshard, y_s.at[p - 1], y_r, row=rr)

    @pl.when(r == holder)
    def _():
        for p in range(1, n_row):
            y_copy(p).start()
        yshard[...] = meas[pl.ds(pl.multiple_of(r * ls + q * lh, 8), lh), pl.ds(yoff, msh)]

    for t in range(1, iters):
        gather_kept(t)
        kept_copies.append(send_kept(t))
    own_big.wait()
    for p in range(1, n_row):
        rr = lax.rem(r + p, n_row)
        k = remote(mat.at[:, pl.ds(pl.multiple_of(rr * wq, LANES), wq)], big.at[r],
                   big_s.at[p - 1], big_r.at[p - 1], row=rr)
        k.start()
        copies.append(k)

    gradient = g0_send[r].astype(F32)
    for k in g0:
        k.wait_recv()
    for p in range(1, n_row):
        gradient = gradient + g0_recv[p - 1].astype(F32)
    current = STEP_SIZE * gradient

    lane = iota((1, LANES), 1)
    shares = jnp.zeros((1, LANES), F32)
    for t in range(iters - 1):
        for k in kept_copies[0] if t == 0 else []:
            k.wait_recv()
        half = current.astype(BF16)
        for rr in range(n_row):
            image = dot(half, kept[t, rr]).astype(BF16)
            for j in range(per):
                pfull[t, rr * per + j] = image[:, j * msh:(j + 1) * msh]
        pair = remote(pfull.at[t, :, pl.ds(pl.multiple_of((1 - q) * lh, 16), lh), :], pair_in.at[t],
                      pair_s.at[t], pair_r.at[t], col=mate)
        pair.start()
        copies.append(pair)
        pair.wait_recv()
        both = pfull[t, :, pl.ds(pl.multiple_of(q * lh, 16), lh), :].astype(F32) + pair_in[t].astype(F32)
        rs_out[t] = both.astype(BF16)
        sends = []
        for p in range(1, n_chip):
            hh = lax.rem(h + p, n_chip)
            k = remote(rs_out.at[t, hh], rs_in.at[t, p - 1], rs_s.at[t, p - 1], rs_r.at[t, p - 1],
                       col=hh * 2 + q)
            k.start()
            sends.append(k)
        predicted = rs_out[t, h].astype(F32)
        if t == 0:
            @pl.when(r != holder)
            def _():
                y_copy(1).wait_recv()
        for p in range(1, n_chip):
            sends[p - 1].wait_recv()
            predicted = predicted + rs_in[t, p - 1].astype(F32)
        copies += sends
        residual = yshard[...] - predicted
        share = jnp.sum(jnp.sum(residual * residual, axis=1, keepdims=True), axis=0, keepdims=True)
        shares = shares + jnp.where(lane == t + 1, share, 0.0)
        rall[t, q, h] = residual.astype(BF16)
        sends = []
        for p in range(1, n_chip):
            hh = lax.rem(h + p, n_chip)
            k = remote(rall.at[t, q, h], rall.at[t, q, h], ag_s.at[t, p - 1], ag_r.at[t, p - 1],
                       col=hh * 2 + q)
            k.start()
            sends.append(k)
        if t == iters - 2:
            en_out[...] = shares
            en_in[c] = shares
            en = []
            for p in range(1, n_col):
                k = remote(en_out, en_in.at[c], en_s.at[p - 1], en_r.at[p - 1],
                           col=lax.rem(c + p, n_col))
                k.start()
                en.append(k)
            copies += en
        for k in sends:
            k.wait_recv()
        copies += sends
        relay = remote(rall.at[t, q], rall.at[t, q], rel_s.at[t], rel_r.at[t], col=mate)
        relay.start()
        copies.append(relay)
        relay.wait_recv()
        if t == iters - 2:
            rx = []
            for p in range(1, n_row):
                k = remote(rall.at[t], rrows.at[p - 1], rx_s.at[p - 1], rx_r.at[p - 1],
                           row=lax.rem(r + p, n_row))
                k.start()
                rx.append(k)
            copies += rx
        full = jnp.concatenate(
            [jnp.concatenate([rall[t, a, b] for b in range(n_chip)], axis=1) for a in range(2)], axis=0)

        def kept_gradient(u):
            return dot_nt(full, jnp.concatenate([kept[u, rr] for rr in range(n_row)], axis=1))

        for k in kept_copies[t + 1]:
            k.wait_recv()
        last = current
        current = carried(current, t) + STEP_SIZE * kept_gradient(t + 1)
    stepped = last + STEP_SIZE * kept_gradient(iters - 2)
    fixed = jnp.sum(stepped * stepped, axis=0, keepdims=True)
    est[...] = pick(current, onehot(iters - 1))

    for k in en:
        k.wait_recv()
    shares = en_in[0]
    for p in range(1, n_col):
        shares = shares + en_in[p]
    shares = shares + jnp.where(lane == 0, energy0, 0.0)

    for k in copies[:n_row - 1]:
        k.wait_recv()
    for k in rx:
        k.wait_recv()
    blocks = [full]
    for p in range(1, n_row):
        blocks.append(jnp.concatenate(
            [jnp.concatenate([rrows[p - 1, a, b] for b in range(n_chip)], axis=1) for a in range(2)], axis=0))
    everyone = jnp.concatenate(blocks, axis=0)
    tile = min(wq, 512)
    for j in range(wq // tile):
        total = jnp.zeros((signals, tile), F32)
        for rr in range(n_row):
            total = total + dot(everyone[:, rr * mb:(rr + 1) * mb], big[rr, :, j * tile:(j + 1) * tile])
        total = STEP_SIZE * total
        fin_out[:, j * tile:(j + 1) * tile] = jnp.sum(total * total, axis=0, keepdims=True)
    fin_out[:, wq:wq + LANES] = fixed
    fin_out[:, wq + LANES:] = shares
    fin_in[r] = fin_out[...]
    fin = []
    for p in range(1, n_row):
        k = remote(fin_out, fin_in.at[r], fin_s.at[p - 1], fin_r.at[p - 1], row=lax.rem(r + p, n_row))
        k.start()
        fin.append(k)
    copies += fin
    for k in fin:
        k.wait_recv()
    ends = fin_in[0, :, wq:]
    for rr in range(1, n_row):
        ends = ends + fin_in[rr, :, wq:]
    as_column = jnp.sum(jnp.where(eye, ends[:, :LANES], 0.0), axis=1, keepdims=True)
    energy[...] = ends[:, LANES:] / (signals * mb * n_row)
    for rr in range(n_row):
        here = index[iters - 2] == iota((KMAX, wq), 1) + rr * wq
        fix = jnp.sum(jnp.where(here, as_column, 0.0), axis=0, keepdims=True)
        mask = jnp.sum(jnp.where(here, 1.0, 0.0), axis=0, keepdims=True)
        norms[:, rr * wq:(rr + 1) * wq] = jnp.sqrt(jnp.where(mask > 0, fix, fin_in[rr, :, :wq]))

    for k in copies:
        k.wait_send()
    for k in g0:
        k.wait_send()
    for group in kept_copies:
        for k in group:
            k.wait_send()

    @pl.when(r == holder)
    def _():
        for p in range(1, n_row):
            y_copy(p).wait_send()


def local(n_row, n_col, matrix, measured, support):
    signals, mb = measured.shape
    width = matrix.shape[1]
    iters = support.shape[0]
    n_chip = n_col // 2
    ls = signals // n_row
    lh = ls // 2
    msh = mb * n_row // n_chip
    wq = width // n_row
    steps = iters - 1
    nr = n_row - 1
    vm = lambda shape, kind: pltpu.VMEM(shape, kind)
    dma = lambda *shape: pltpu.SemaphoreType.DMA(shape)
    scratch = [
        vm((iters, n_row, KMAX, mb), BF16),
        vm((n_row, ls, KMAX), BF16),
        vm((nr, ls, KMAX), BF16),
        vm((lh, msh), F32),
        vm((n_row, mb, wq), BF16),
        vm((steps, n_chip, ls, msh), BF16),
        vm((steps, n_chip, lh, msh), BF16),
        vm((steps, n_chip, lh, msh), BF16),
        vm((steps, n_chip - 1, lh, msh), BF16),
        vm((steps, 2, n_chip, lh, msh), BF16),
        vm((nr, 2, n_chip, lh, msh), BF16),
        vm((1, LANES), F32),
        vm((n_col, 1, LANES), F32),
        vm((1, wq + 2 * LANES), F32),
        vm((n_row, 1, wq + 2 * LANES), F32),
        dma(iters, nr), dma(iters, nr), dma(nr), dma(nr), dma(nr), pltpu.SemaphoreType.DMA,
        dma(nr), dma(nr), pltpu.SemaphoreType.DMA,
        dma(steps), dma(steps), dma(steps, n_chip - 1), dma(steps, n_chip - 1),
        dma(steps, n_chip - 1), dma(steps, n_chip - 1), dma(steps), dma(steps),
        dma(nr), dma(nr), dma(n_col - 1), dma(n_col - 1), dma(nr), dma(nr),
    ]
    vmem = pl.BlockSpec(memory_space=pltpu.VMEM)
    est, norms, energy = pl.pallas_call(
        functools.partial(kernel, n_row, n_col),
        out_shape=(
            jax.ShapeDtypeStruct((ls, width), F32),
            jax.ShapeDtypeStruct((1, width), F32),
            jax.ShapeDtypeStruct((1, LANES), F32),
        ),
        in_specs=[vmem] * 3,
        out_specs=(vmem,) * 3,
        scratch_shapes=scratch,
        compiler_params=pltpu.CompilerParams(
            collective_id=0, has_side_effects=True, vmem_limit_bytes=60 * 2**20),
    )(matrix, measured, support)
    return est, norms.reshape(width), energy[0, :iters]


def solution(mesh):
    placed = (P("row", "col"), P(None, "row"), P())
    return jax.shard_map(
        functools.partial(local, mesh.shape["row"], mesh.shape["col"]),
        mesh=mesh,
        in_specs=placed,
        out_specs=(P("row", "col"), P("col"), P()),
        check_vma=False,
    )
```

time: 429 us -> 86.6 us (0.20)
  waiting for transfers between devices: 364 us -> 0 us
  Pallas kernels: 0 us -> 81 us
  matrix products: 30.6 us -> 0 us
  between operations: 14.2 us -> 0.64 us
  other arithmetic: 7.66 us -> 0 us
  blocking collectives: 7.1 us -> 0 us
    psum x6 -> x0, waiting for transfers between devices: 334 us -> none  [the longest x3 269 us: local(): lax.psum(image.astype(jnp.bfloat16), 'col').astype(jnp.float32)]
    pallas_call x0 -> x1, Pallas kernels: none -> 81 us  [local(): pl.pallas_call(functools.partial(kernel, n_row, n_col), out_shape=(jax.Sh...]
    dot_general x13 -> x0, matrix products: 30.6 us -> none  [the longest x3 11.1 us: local(): lax.dot_general(e, matrix, NT, preferred_element_type=jnp.float32)]
    reduce_scatter x1 -> x0, waiting for transfers between devices: 30.5 us -> none  [local(): lax.psum_scatter(jnp.dot(half, matrix, preferred_element_type=jnp.float32...]
    psum x1 -> x0, blocking collectives: 7.1 us -> none  [local(): sums = lax.psum(sums, 'row')]
  transfers between devices with their start and end apart: 7 -> 0, of which waited for: 7 -> 0; matrix products, arithmetic and copies ran while one was open for 2% -> 0% of each run, Pallas kernels for 0% -> 0%
where the time goes in v2:
time: 86.6 us; the launch traced here: 86.4 us
  Pallas kernels  81 us (94%)
  local copies, waits for them, and re-layouts  4.82 us (6%)
    pallas_call x1, Pallas kernels, local(): pl.pallas_call(functools.partial(kernel, n_row, n_col), out_shape=(jax.Sh...  81 us
    unnamed x4, local copies, waits for them, and re-layouts  3.73 us

profile of v2, /device:TPU:0, one launch (start us, length us, event | category | flops | bytes accessed | tf_op | source)
XLA Modules:
  0.0 86.4 jit_solution(17293874118461691750)
XLA Ops:
  0.6 81.0 %shard_map.58 = (f32[128,4096]{1,0:T(8,128)}, f32[1,4096]{1,0:T(1,128)}, f32[1,128]{1,0:T(1,128)}) custom-call(bf16[512,4096]{1,0:T(8,128)(2,1)} %mat.1, f32[256,512]{1,0:T(8,128)} %meas.1, s32[4,1024]{1,0:T(4,128)} %sup.1), custom_call_target="tpu_custom_call" | custom-call | tf_op jit(solution)/shard_map/pallas_call | solution.py:330
  81.6 1.1 %slice_bitcast_fusion = f32[4]{0:T(128)} fusion(f32[1,128]{1,0:T(1,128)} %get-tuple-element.8), kind=kLoop, calls=%fused_computation | loop fusion | bytes 32 | tf_op jit(solution)/shard_map/squeeze | solution.py:343
  82.7 0.0 copy-start
  82.7 3.1 %copy.8 = f32[128,4096]{1,0:T(8,128)} copy(f32[128,4096]{1,0:T(8,128)} %get-tuple-element.12) | data formatting | bytes 4194304
  85.8 0.0 copy-done
  85.8 0.6 copy.9
Async XLA Ops:
  82.7 3.1 %copy-start = (f32[1,4096]{1,0:T(1,128)S(1)}, f32[1,4096]{1,0:T(1,128)}, u32[]{:S(2)}) copy-start(f32[1,4096]{1,0:T(1,128)} %get-tuple-element.7) | copy-start | bytes 49156

commit v3 on v2

--- a/solution.py
+++ b/solution.py
@@ -35,12 +35,16 @@
     return lax.broadcasted_iota(jnp.int32, shape, axis).astype(F32)
 
 
-def kernel(n_row, n_col, mat, meas, sup, est, norms, energy,
+def ahead(columns):
+    return columns - columns * 5 // 16 // LANES * LANES
+
+
+def kernel(n_row, n_col, mat, meas, sup, chosen, where_to, norms, energy,
            kept, g0_send, g0_recv, yshard, big, pfull, pair_in, rs_out, rs_in,
-           rall, rrows, en_out, en_in, fin_out, fin_in,
+           rall, rrows, en_out, en_in, fin_out, fin_in, gsend, grecv,
            kept_s, kept_r, g0_s, g0_r, y_s, y_r, big_s, big_r, loc,
            pair_s, pair_r, rs_s, rs_r, ag_s, ag_r, rel_s, rel_r, rx_s, rx_r,
-           en_s, en_r, fin_s, fin_r):
+           en_s, en_r, fin_s, fin_r, grad_s, grad_r):
     r, c = lax.axis_index("row"), lax.axis_index("col")
     n_chip = n_col // 2
     q, h = lax.rem(c, 2), lax.div(c, 2)
@@ -52,6 +56,7 @@
     lh = ls // 2
     msh = mb * n_row // n_chip
     wq = width // n_row
+    wp = ahead(wq)
     per = mb // msh
 
     def remote(src, dst, s, d, row=None, col=None):
@@ -66,7 +71,7 @@
     for p in range(1, n_col):
         pl.semaphore_signal(barrier, inc=1, device_id=(r, lax.rem(c + p, n_col)), device_id_type=MESH)
 
-    own_big = pltpu.make_async_copy(mat.at[:, pl.ds(pl.multiple_of(r * wq, LANES), wq)], big.at[r], loc)
+    own_big = pltpu.make_async_copy(mat.at[:, pl.ds(pl.multiple_of(r * wq, LANES), wp)], big.at[r], loc)
     own_big.start()
 
     offset = (c * width).astype(F32)
@@ -137,7 +142,7 @@
     own_big.wait()
     for p in range(1, n_row):
         rr = lax.rem(r + p, n_row)
-        k = remote(mat.at[:, pl.ds(pl.multiple_of(rr * wq, LANES), wq)], big.at[r],
+        k = remote(mat.at[:, pl.ds(pl.multiple_of(rr * wq, LANES), wp)], big.at[r],
                    big_s.at[p - 1], big_r.at[p - 1], row=rr)
         k.start()
         copies.append(k)
@@ -150,6 +155,7 @@
     current = STEP_SIZE * gradient
 
     lane = iota((1, LANES), 1)
+    far = sorted(range(1, n_chip), key=lambda p: min(p, n_chip - p), reverse=True)
     shares = jnp.zeros((1, LANES), F32)
     for t in range(iters - 1):
         for k in kept_copies[0] if t == 0 else []:
@@ -167,7 +173,7 @@
         both = pfull[t, :, pl.ds(pl.multiple_of(q * lh, 16), lh), :].astype(F32) + pair_in[t].astype(F32)
         rs_out[t] = both.astype(BF16)
         sends = []
-        for p in range(1, n_chip):
+        for p in far:
             hh = lax.rem(h + p, n_chip)
             k = remote(rs_out.at[t, hh], rs_in.at[t, p - 1], rs_s.at[t, p - 1], rs_r.at[t, p - 1],
                        col=hh * 2 + q)
@@ -178,8 +184,8 @@
             @pl.when(r != holder)
             def _():
                 y_copy(1).wait_recv()
-        for p in range(1, n_chip):
-            sends[p - 1].wait_recv()
+        for p, k in zip(reversed(far), reversed(sends)):
+            k.wait_recv()
             predicted = predicted + rs_in[t, p - 1].astype(F32)
         copies += sends
         residual = yshard[...] - predicted
@@ -187,7 +193,7 @@
         shares = shares + jnp.where(lane == t + 1, share, 0.0)
         rall[t, q, h] = residual.astype(BF16)
         sends = []
-        for p in range(1, n_chip):
+        for p in far:
             hh = lax.rem(h + p, n_chip)
             k = remote(rall.at[t, q, h], rall.at[t, q, h], ag_s.at[t, p - 1], ag_r.at[t, p - 1],
                        col=hh * 2 + q)
@@ -230,7 +236,27 @@
         current = carried(current, t) + STEP_SIZE * kept_gradient(t + 1)
     stepped = last + STEP_SIZE * kept_gradient(iters - 2)
     fixed = jnp.sum(stepped * stepped, axis=0, keepdims=True)
-    est[...] = pick(current, onehot(iters - 1))
+    chosen[...] = current
+    where_to[...] = jnp.broadcast_to(index[iters - 1], (KMAX, KMAX))
+
+    def partial_gradients(m, block):
+        sig = lax.rem(r - m + n_row, n_row)
+        held = jnp.concatenate(
+            [jnp.concatenate([block(a, r * per + j) for j in range(per)], axis=1) for a in range(2)], axis=0)
+        for rr in range(n_row):
+            cols = slice(rr * wq + wp, (rr + 1) * wq)
+            gsend[rr, sig] = dot(held, mat[:, cols]).astype(BF16)
+        for p in range(1, n_row):
+            rr = lax.rem(r + p, n_row)
+            k = remote(gsend.at[rr, sig], grecv.at[p - 1, sig], grad_s.at[p - 1, m], grad_r.at[p - 1, m], row=rr)
+            k.start()
+            grads.append(k)
+
+    grads = []
+    partial_gradients(0, lambda a, b: rall[iters - 2, a, b])
+    for p in range(1, n_row):
+        rx[p - 1].wait_recv()
+        partial_gradients(p, lambda a, b: rrows[p - 1, a, b])
 
     for k in en:
         k.wait_recv()
@@ -241,20 +267,29 @@
 
     for k in copies[:n_row - 1]:
         k.wait_recv()
-    for k in rx:
-        k.wait_recv()
     blocks = [full]
     for p in range(1, n_row):
         blocks.append(jnp.concatenate(
             [jnp.concatenate([rrows[p - 1, a, b] for b in range(n_chip)], axis=1) for a in range(2)], axis=0))
     everyone = jnp.concatenate(blocks, axis=0)
-    tile = min(wq, 512)
-    for j in range(wq // tile):
-        total = jnp.zeros((signals, tile), F32)
-        for rr in range(n_row):
-            total = total + dot(everyone[:, rr * mb:(rr + 1) * mb], big[rr, :, j * tile:(j + 1) * tile])
+    for j in range(0, wp, 512):
+        cols = slice(j, min(j + 512, wp))
+        total = dot(everyone[:, :mb], big[0, :, cols])
+        for rr in range(1, n_row):
+            total = total + dot(everyone[:, rr * mb:(rr + 1) * mb], big[rr, :, cols])
         total = STEP_SIZE * total
-        fin_out[:, j * tile:(j + 1) * tile] = jnp.sum(total * total, axis=0, keepdims=True)
+        fin_out[:, cols] = jnp.sum(total * total, axis=0, keepdims=True)
+    for k in grads:
+        k.wait_recv()
+    copies += grads
+    tail = jnp.zeros((1, wq - wp), F32)
+    for sig in range(n_row):
+        total = gsend[r, sig].astype(F32)
+        for p in range(1, n_row):
+            total = total + grecv[p - 1, sig].astype(F32)
+        total = STEP_SIZE * total
+        tail = tail + jnp.sum(total * total, axis=0, keepdims=True)
+    fin_out[:, wp:wq] = tail
     fin_out[:, wq:wq + LANES] = fixed
     fin_out[:, wq + LANES:] = shares
     fin_in[r] = fin_out[...]
@@ -291,6 +326,17 @@
             y_copy(p).wait_send()
 
 
+def expand(chosen, where_to, norms, est, flat):
+    tile = est.shape[1]
+    start = (pl.program_id(0) * tile).astype(F32)
+    hit = where_to[:, :1] - start == iota((KMAX, tile), 1)
+    est[...] = pick(chosen[...], jnp.where(hit, 1.0, 0.0).astype(BF16))
+
+    @pl.when(pl.program_id(0) == 0)
+    def _():
+        flat[...] = norms[...].reshape(flat.shape)
+
+
 def local(n_row, n_col, matrix, measured, support):
     signals, mb = measured.shape
     width = matrix.shape[1]
@@ -300,6 +346,7 @@
     lh = ls // 2
     msh = mb * n_row // n_chip
     wq = width // n_row
+    wp = ahead(wq)
     steps = iters - 1
     nr = n_row - 1
     vm = lambda shape, kind: pltpu.VMEM(shape, kind)
@@ -309,7 +356,7 @@
         vm((n_row, ls, KMAX), BF16),
         vm((nr, ls, KMAX), BF16),
         vm((lh, msh), F32),
-        vm((n_row, mb, wq), BF16),
+        vm((n_row, mb, wp), BF16),
         vm((steps, n_chip, ls, msh), BF16),
         vm((steps, n_chip, lh, msh), BF16),
         vm((steps, n_chip, lh, msh), BF16),
@@ -320,27 +367,46 @@
         vm((n_col, 1, LANES), F32),
         vm((1, wq + 2 * LANES), F32),
         vm((n_row, 1, wq + 2 * LANES), F32),
+        vm((n_row, n_row, ls, wq - wp), BF16),
+        vm((nr, n_row, ls, wq - wp), BF16),
         dma(iters, nr), dma(iters, nr), dma(nr), dma(nr), dma(nr), pltpu.SemaphoreType.DMA,
         dma(nr), dma(nr), pltpu.SemaphoreType.DMA,
         dma(steps), dma(steps), dma(steps, n_chip - 1), dma(steps, n_chip - 1),
         dma(steps, n_chip - 1), dma(steps, n_chip - 1), dma(steps), dma(steps),
         dma(nr), dma(nr), dma(n_col - 1), dma(n_col - 1), dma(nr), dma(nr),
+        dma(nr, n_row), dma(nr, n_row),
     ]
     vmem = pl.BlockSpec(memory_space=pltpu.VMEM)
-    est, norms, energy = pl.pallas_call(
+    chosen, where_to, norms, energy = pl.pallas_call(
         functools.partial(kernel, n_row, n_col),
         out_shape=(
-            jax.ShapeDtypeStruct((ls, width), F32),
+            jax.ShapeDtypeStruct((ls, KMAX), F32),
+            jax.ShapeDtypeStruct((KMAX, KMAX), F32),
             jax.ShapeDtypeStruct((1, width), F32),
             jax.ShapeDtypeStruct((1, LANES), F32),
         ),
         in_specs=[vmem] * 3,
-        out_specs=(vmem,) * 3,
+        out_specs=(vmem,) * 4,
         scratch_shapes=scratch,
         compiler_params=pltpu.CompilerParams(
             collective_id=0, has_side_effects=True, vmem_limit_bytes=60 * 2**20),
     )(matrix, measured, support)
-    return est, norms.reshape(width), energy[0, :iters]
+    tile = 512
+    est, flat = pl.pallas_call(
+        expand,
+        grid=(width // tile,),
+        out_shape=(jax.ShapeDtypeStruct((ls, width), F32), jax.ShapeDtypeStruct((width,), F32)),
+        in_specs=[
+            pl.BlockSpec((ls, KMAX), lambda j: (0, 0)),
+            pl.BlockSpec((KMAX, KMAX), lambda j: (0, 0)),
+            pl.BlockSpec((1, width), lambda j: (0, 0)),
+        ],
+        out_specs=(
+            pl.BlockSpec((ls, tile), lambda j: (0, j)),
+            pl.BlockSpec((width,), lambda j: (0,)),
+        ),
+    )(chosen, where_to, norms)
+    return est, flat, energy[0, :iters]
 
 
 def solution(mesh):

time: 86.6 us -> 79.4 us (0.917)
  local copies, waits for them, and re-layouts: 4.82 us -> 1.14 us
  Pallas kernels: 81 us -> 77.4 us
    pallas_call x1, Pallas kernels: 81 us -> 72.1 us  [local(): pl.pallas_call(functools.partial(kernel, n_row, n_col), out_shape=(jax.Sh...]
    pallas_call x0 -> x1, Pallas kernels: none -> 5.33 us  [local(): pl.pallas_call(expand, grid=(width // tile,), out_shape=(jax.ShapeDtypeSt...]
    unnamed x4 -> x0, local copies, waits for them, and re-layouts: 3.73 us -> none
where the time goes in v3:
time: 79.4 us; the launch traced here: 79.2 us
  Pallas kernels  77.4 us (97%)
  local copies, waits for them, and re-layouts  1.14 us (1%)
    pallas_call x1, Pallas kernels, local(): pl.pallas_call(functools.partial(kernel, n_row, n_col), out_shape=(jax.Sh...  72.1 us
    pallas_call x1, Pallas kernels, local(): pl.pallas_call(expand, grid=(width // tile,), out_shape=(jax.ShapeDtypeSt...  5.33 us

profile of v3, /device:TPU:0, one launch (start us, length us, event | category | flops | bytes accessed | tf_op | source)
XLA Modules:
  0.0 79.2 jit_solution(5248278067917757272)
XLA Ops:
  0.6 72.1 %shard_map.58 = (f32[128,128]{1,0:T(8,128)}, f32[128,128]{1,0:T(8,128)}, f32[1,4096]{1,0:T(1,128)}, f32[1,128]{1,0:T(1,128)}) custom-call(bf16[512,4096]{1,0:T(8,128)(2,1)} %mat.1, f32[256,512]{1,0:T(8,128)} %meas.1, s32[4,1024]{1,0:T(4,128)} %sup.1), custom_call_target="tpu_custom_call" | custom-call | tf_op jit(solution)/shard_map/pallas_call | solution.py:380
  72.7 1.1 %slice_bitcast_fusion = f32[4]{0:T(128)} fusion(f32[1,128]{1,0:T(1,128)} %get-tuple-element.14), kind=kLoop, calls=%fused_computation | loop fusion | bytes 32 | tf_op jit(solution)/shard_map/squeeze | solution.py:409
  73.9 5.3 %shard_map.59 = (f32[128,4096]{1,0:T(8,128)}, f32[4096]{0:T(1024)}) custom-call(f32[128,128]{1,0:T(8,128)} %get-tuple-element.9.chosen, f32[128,128]{1,0:T(8,128)} %get-tuple-element.10.where_to, f32[1,4096]{1,0:T(1,128)} %get-tuple-element.11.norms), custom_call_target="tpu_custom_call" | custom-call | tf_op jit(solution)/shard_map/pallas_call | solution.py:395

commit v4 on v3

--- a/solution.py
+++ b/solution.py
@@ -44,7 +44,7 @@
            rall, rrows, en_out, en_in, fin_out, fin_in, gsend, grecv,
            kept_s, kept_r, g0_s, g0_r, y_s, y_r, big_s, big_r, loc,
            pair_s, pair_r, rs_s, rs_r, ag_s, ag_r, rel_s, rel_r, rx_s, rx_r,
-           en_s, en_r, fin_s, fin_r, grad_s, grad_r):
+           en_s, en_r, fin_s, fin_r, grad_s, grad_r, mate_s, mate_r):
     r, c = lax.axis_index("row"), lax.axis_index("col")
     n_chip = n_col // 2
     q, h = lax.rem(c, 2), lax.div(c, 2)
@@ -136,16 +136,23 @@
             y_copy(p).start()
         yshard[...] = meas[pl.ds(pl.multiple_of(r * ls + q * lh, 8), lh), pl.ds(yoff, msh)]
 
-    for t in range(1, iters):
+    bulk = []
+
+    def send_ahead(piece):
+        rows = pl.ds(piece * (mb // iters), mb // iters)
+        for p in range(1, n_row):
+            rr = lax.rem(r + p, n_row)
+            k = remote(mat.at[rows, pl.ds(pl.multiple_of(rr * wq, LANES), wp)], big.at[r, rows],
+                       big_s.at[p - 1, piece], big_r.at[p - 1, piece], row=rr)
+            k.start()
+            bulk.append(k)
+
+    def further(t):
         gather_kept(t)
         kept_copies.append(send_kept(t))
-    own_big.wait()
-    for p in range(1, n_row):
-        rr = lax.rem(r + p, n_row)
-        k = remote(mat.at[:, pl.ds(pl.multiple_of(rr * wq, LANES), wp)], big.at[r],
-                   big_s.at[p - 1], big_r.at[p - 1], row=rr)
-        k.start()
-        copies.append(k)
+        send_ahead(t)
+
+    send_ahead(0)
 
     gradient = g0_send[r].astype(F32)
     for k in g0:
@@ -157,6 +164,20 @@
     lane = iota((1, LANES), 1)
     far = sorted(range(1, n_chip), key=lambda p: min(p, n_chip - p), reverse=True)
     shares = jnp.zeros((1, LANES), F32)
+
+    def partial_gradients(grads, m, block):
+        sig = lax.rem(r - m + n_row, n_row)
+        held = jnp.concatenate(
+            [jnp.concatenate([block(a, r * per + j) for j in range(per)], axis=1) for a in range(2)], axis=0)
+        for rr in range(n_row):
+            cols = slice(rr * wq + wp, (rr + 1) * wq)
+            gsend[rr, sig] = dot(held, mat[:, cols]).astype(BF16)
+        for p in range(1, n_row):
+            rr = lax.rem(r + p, n_row)
+            k = remote(gsend.at[rr, sig], grecv.at[p - 1, sig], grad_s.at[p - 1, m], grad_r.at[p - 1, m], row=rr)
+            k.start()
+            grads.append(k)
+
     for t in range(iters - 1):
         for k in kept_copies[0] if t == 0 else []:
             k.wait_recv()
@@ -179,6 +200,8 @@
                        col=hh * 2 + q)
             k.start()
             sends.append(k)
+        if t == 0:
+            further(1)
         predicted = rs_out[t, h].astype(F32)
         if t == 0:
             @pl.when(r != holder)
@@ -199,6 +222,9 @@
                        col=hh * 2 + q)
             k.start()
             sends.append(k)
+        if t == 0:
+            for u in range(2, iters):
+                further(u)
         if t == iters - 2:
             en_out[...] = shares
             en_in[c] = shares
@@ -212,18 +238,21 @@
         for k in sends:
             k.wait_recv()
         copies += sends
+        if t == iters - 2:
+            rx = []
+            for p in range(1, n_row):
+                k = remote(rall.at[t, q], rrows.at[p - 1, q], rx_s.at[p - 1], rx_r.at[p - 1],
+                           row=lax.rem(r + p, n_row))
+                k.start()
+                rx.append(k)
+            copies += rx
         relay = remote(rall.at[t, q], rall.at[t, q], rel_s.at[t], rel_r.at[t], col=mate)
         relay.start()
         copies.append(relay)
         relay.wait_recv()
         if t == iters - 2:
-            rx = []
-            for p in range(1, n_row):
-                k = remote(rall.at[t], rrows.at[p - 1], rx_s.at[p - 1], rx_r.at[p - 1],
-                           row=lax.rem(r + p, n_row))
-                k.start()
-                rx.append(k)
-            copies += rx
+            grads = []
+            partial_gradients(grads, 0, lambda a, b: rall[t, a, b])
         full = jnp.concatenate(
             [jnp.concatenate([rall[t, a, b] for b in range(n_chip)], axis=1) for a in range(2)], axis=0)
 
@@ -239,24 +268,13 @@
     chosen[...] = current
     where_to[...] = jnp.broadcast_to(index[iters - 1], (KMAX, KMAX))
 
-    def partial_gradients(m, block):
-        sig = lax.rem(r - m + n_row, n_row)
-        held = jnp.concatenate(
-            [jnp.concatenate([block(a, r * per + j) for j in range(per)], axis=1) for a in range(2)], axis=0)
-        for rr in range(n_row):
-            cols = slice(rr * wq + wp, (rr + 1) * wq)
-            gsend[rr, sig] = dot(held, mat[:, cols]).astype(BF16)
-        for p in range(1, n_row):
-            rr = lax.rem(r + p, n_row)
-            k = remote(gsend.at[rr, sig], grecv.at[p - 1, sig], grad_s.at[p - 1, m], grad_r.at[p - 1, m], row=rr)
-            k.start()
-            grads.append(k)
-
-    grads = []
-    partial_gradients(0, lambda a, b: rall[iters - 2, a, b])
     for p in range(1, n_row):
         rx[p - 1].wait_recv()
-        partial_gradients(p, lambda a, b: rrows[p - 1, a, b])
+        k = remote(rrows.at[p - 1, q], rrows.at[p - 1, q], mate_s.at[p - 1], mate_r.at[p - 1], col=mate)
+        k.start()
+        copies.append(k)
+        k.wait_recv()
+        partial_gradients(grads, p, lambda a, b: rrows[p - 1, a, b])
 
     for k in en:
         k.wait_recv()
@@ -265,8 +283,10 @@
         shares = shares + en_in[p]
     shares = shares + jnp.where(lane == 0, energy0, 0.0)
 
-    for k in copies[:n_row - 1]:
-        k.wait_recv()
+    own_big.wait()
+    for k in bulk:
+        k.wait_recv()
+    copies += bulk
     blocks = [full]
     for p in range(1, n_row):
         blocks.append(jnp.concatenate(
@@ -326,7 +346,7 @@
             y_copy(p).wait_send()
 
 
-def expand(chosen, where_to, norms, est, flat):
+def expand(chosen, where_to, norms, sums, est, flat, energy):
     tile = est.shape[1]
     start = (pl.program_id(0) * tile).astype(F32)
     hit = where_to[:, :1] - start == iota((KMAX, tile), 1)
@@ -335,6 +355,8 @@
     @pl.when(pl.program_id(0) == 0)
     def _():
         flat[...] = norms[...].reshape(flat.shape)
+        for i in range(energy.shape[0]):
+            energy[i] = sums[0, i]
 
 
 def local(n_row, n_col, matrix, measured, support):
@@ -370,11 +392,11 @@
         vm((n_row, n_row, ls, wq - wp), BF16),
         vm((nr, n_row, ls, wq - wp), BF16),
         dma(iters, nr), dma(iters, nr), dma(nr), dma(nr), dma(nr), pltpu.SemaphoreType.DMA,
-        dma(nr), dma(nr), pltpu.SemaphoreType.DMA,
+        dma(nr, iters), dma(nr, iters), pltpu.SemaphoreType.DMA,
         dma(steps), dma(steps), dma(steps, n_chip - 1), dma(steps, n_chip - 1),
         dma(steps, n_chip - 1), dma(steps, n_chip - 1), dma(steps), dma(steps),
         dma(nr), dma(nr), dma(n_col - 1), dma(n_col - 1), dma(nr), dma(nr),
-        dma(nr, n_row), dma(nr, n_row),
+        dma(nr, n_row), dma(nr, n_row), dma(nr), dma(nr),
     ]
     vmem = pl.BlockSpec(memory_space=pltpu.VMEM)
     chosen, where_to, norms, energy = pl.pallas_call(
@@ -392,21 +414,23 @@
             collective_id=0, has_side_effects=True, vmem_limit_bytes=60 * 2**20),
     )(matrix, measured, support)
     tile = 512
-    est, flat = pl.pallas_call(
+    return pl.pallas_call(
         expand,
         grid=(width // tile,),
-        out_shape=(jax.ShapeDtypeStruct((ls, width), F32), jax.ShapeDtypeStruct((width,), F32)),
+        out_shape=(jax.ShapeDtypeStruct((ls, width), F32), jax.ShapeDtypeStruct((width,), F32),
+                   jax.ShapeDtypeStruct((iters,), F32)),
         in_specs=[
             pl.BlockSpec((ls, KMAX), lambda j: (0, 0)),
             pl.BlockSpec((KMAX, KMAX), lambda j: (0, 0)),
             pl.BlockSpec((1, width), lambda j: (0, 0)),
+            pl.BlockSpec(memory_space=pltpu.SMEM),
         ],
         out_specs=(
             pl.BlockSpec((ls, tile), lambda j: (0, j)),
             pl.BlockSpec((width,), lambda j: (0,)),
+            pl.BlockSpec(memory_space=pltpu.SMEM),
         ),
-    )(chosen, where_to, norms)
-    return est, flat, energy[0, :iters]
+    )(chosen, where_to, norms, energy)
 
 
 def solution(mesh):

time: 79.4 us -> 75.3 us (0.948)
  Pallas kernels: 77.4 us -> 74.5 us
  local copies, waits for them, and re-layouts: 1.14 us -> 0 us
    pallas_call x1, Pallas kernels: 72.1 us -> 69 us  [local(): pl.pallas_call(functools.partial(kernel, n_row, n_col), out_shape=(jax.Sh...]
    squeeze x1 -> x0, local copies, waits for them, and re-layouts: 1.14 us -> none  [local(): return (est, flat, energy[0, :iters])]
where the time goes in v4:
time: 75.3 us; the launch traced here: 75.1 us
  Pallas kernels  74.5 us (99%)
    pallas_call x1, Pallas kernels, local(): pl.pallas_call(functools.partial(kernel, n_row, n_col), out_shape=(jax.Sh...  69 us
    pallas_call x1, Pallas kernels, local(): pl.pallas_call(expand, grid=(width // tile,), out_shape=(jax.ShapeDtypeSt...  5.43 us

profile of v4, /device:TPU:0, one launch (start us, length us, event | category | flops | bytes accessed | tf_op | source)
XLA Modules:
  0.0 75.1 jit_solution(7956363193804513654)
XLA Ops:
  0.6 69.0 %shard_map.58 = (f32[128,128]{1,0:T(8,128)}, f32[128,128]{1,0:T(8,128)}, f32[1,4096]{1,0:T(1,128)}, f32[1,128]{1,0:T(1,128)}) custom-call(bf16[512,4096]{1,0:T(8,128)(2,1)} %mat.1, f32[256,512]{1,0:T(8,128)} %meas.1, s32[4,1024]{1,0:T(4,128)} %sup.1), custom_call_target="tpu_custom_call" | custom-call | tf_op jit(solution)/shard_map/pallas_call | solution.py:402
  69.7 5.4 %shard_map.59 = (f32[128,4096]{1,0:T(8,128)}, f32[4096]{0:T(1024)}, f32[4]{0:T(128)}) custom-call(f32[128,128]{1,0:T(8,128)} %get-tuple-element.7.chosen, f32[128,128]{1,0:T(8,128)} %get-tuple-element.8.where_to, f32[1,4096]{1,0:T(1,128)} %get-tuple-element.9.norms, f32[1,128]{1,0:T(1,128)} %get-tuple-element.10.sums), custom_call_target="tpu_custom_call" | custom-call | tf_op jit(solution)/shard_map/pallas_call | solution.py:417
